TPU v7x, 32 devices: a whole 2x2x4 slice. The times are simulated.
32 devices in a mesh: grp: 4 (over y, x), row: 8 (over z, core).
Axes of the slice: x: 2, y: 2, z: 4, core: 2. Of those that a mesh axis runs over, the one named last changes fastest.
Arguments:
- serving: bfloat16 [16384, 128], P('row'), may hold values from -1 to 1
- serving_scale: bfloat16 [128], P('row'), may hold values from 0.099609375 to 1
- hot_blocks: int32 [4, 16], P('grp', 'row'), may hold values from 0 to 15, as said below
- bag_lengths: int32 [32, 256], P(('grp', 'row')), may hold values from 1 to 16, 1024 in all within a row
- bag_indices: int32 [32, 1024], P(('grp', 'row')), may hold values from 0 to 2047, as said below
- dense_act: bfloat16 [8192, 128], P(('grp', 'row')), may hold values from -6 to 6
- labels: float32 [8192], P(('grp', 'row')), may hold values from 0 to 1
- w_top: bfloat16 [256, 1024], replicated, may hold values from -0.375 to 0.375
- w_out: float32 [1024], replicated, may hold values from -0.012 to 0.012
- master: float32 [4, 4096, 128], P('grp', 'row'), may hold values from -0.3 to 0.3
- accum: float32 [4, 4096], P('grp', 'row'), may hold values from 1e-05 to 0.0001
Outputs:
- new_master: float32 [4, 4096, 128], P('grp', 'row')
- new_accum: float32 [4, 4096], P('grp', 'row')
- new_serving: bfloat16 [16384, 128], P('row')
- new_scale: bfloat16 [128], P('row')
- top_grad: float32 [256, 1024], replicated
Inputs may be any that keep to these rules, and one draw needn't show every extreme that they name: `hot_blocks`: the 2 entries that one group names in one row shard are distinct. `bag_indices`: in each device's line, exactly 64 distinct values lie in each range of 256 consecutive positions that starts at a multiple of 256.
All inputs are finite; a program needn't handle non-finite values. Where the computation divides by a largest or mean magnitude, that divisor is 1e-20 or more.
Results may differ from a plain program's by a relative error of at most 0.012.
Values may be sent and summed in bfloat16 or wider, within the bound.
A program may use at most 128 MiB of HBM per device.

v0:
```python
import math
import jax
import jax.numpy as jnp
from jax import lax
from jax.sharding import PartitionSpec as P

BLOCK = 128
MOST = 16
lr_step = 0.05


def pool_grad(table, lengths, indices, dense_d, labels_d, w_top, w_out):
    rows, width = table.shape
    total = indices.shape[0]
    ends = jnp.cumsum(lengths)
    starts = ends - lengths
    slots = jnp.arange(MOST, dtype=jnp.int32)
    positions = jnp.minimum(starts[:, None] + slots[None, :], total - 1)
    picked = jnp.where(slots[None, :] < lengths[:, None], indices[positions], -1)
    span = math.gcd(rows, 2048)
    pieces = rows // span

    def count_block(first):
        columns = first + jnp.arange(span, dtype=jnp.int32)
        return jnp.sum((picked[:, :, None] == columns[None, None, :]).astype(jnp.bfloat16), axis=1)

    counts = lax.map(count_block, jnp.arange(pieces, dtype=jnp.int32) * span)
    table_blocks = table.reshape(pieces, span, width)

    def add_block(running, pair):
        block_counts, block_rows = pair
        return (
            running
            + jnp.dot(
                block_counts.astype(jnp.float32), block_rows, precision=lax.Precision.HIGHEST
            ),
            None,
        )

    pooled, _ = lax.scan(
        add_block, jnp.zeros((lengths.shape[0], width), jnp.float32), (counts, table_blocks)
    )
    joined = jnp.concatenate([pooled.astype(jnp.bfloat16), dense_d], axis=1)
    pre = jnp.dot(joined, w_top, preferred_element_type=jnp.float32)
    sig = jax.nn.sigmoid(pre)
    logit = jnp.dot(pre * sig, w_out, precision=lax.Precision.HIGHEST)
    dlogit = jax.nn.sigmoid(logit) - labels_d
    dpre = (dlogit[:, None] * w_out[None, :] * (sig * (1.0 + pre * (1.0 - sig)))).astype(
        jnp.bfloat16
    )
    top = lax.dot_general(
        joined, dpre, (((0,), (0,)), ((), ())), preferred_element_type=jnp.float32
    )
    dz = lax.dot_general(dpre, w_top, (((1,), (1,)), ((), ())), preferred_element_type=jnp.float32)
    emb_grad = dz[:, :width]

    def spread_block(block_counts):
        weights = block_counts.astype(jnp.float32)
        summed = lax.dot_general(
            weights, emb_grad, (((0,), (0,)), ((), ())), precision=lax.Precision.HIGHEST
        )
        return (summed, jnp.sum(weights, axis=0))

    hot, column_use = lax.map(spread_block, counts)
    return (top, hot.reshape(rows, width), column_use.reshape(rows) > 0)


def on_device(
    serving,
    serving_scale,
    hot_blocks,
    bag_lengths,
    bag_indices,
    dense_act,
    labels,
    w_top,
    w_out,
    master,
    accum,
):
    width = serving.shape[1]
    chosen = hot_blocks[0]
    count = chosen.shape[0]
    local_blocks = serving.reshape(-1, BLOCK, width)
    total_blocks = local_blocks.shape[0]
    picked = local_blocks[chosen]
    picked_scale = serving_scale[chosen]
    fetched, fetched_scale = (
        lax.all_gather(picked, "row", axis=0, tiled=True),
        lax.all_gather(picked_scale, "row", axis=0, tiled=True),
    )
    table = (
        fetched.astype(jnp.float32) * fetched_scale.astype(jnp.float32)[:, None, None]
    ).reshape(-1, width)
    top_part, hot_part, used_rows = pool_grad(
        table, bag_lengths[0], bag_indices[0], dense_act, labels, w_top, w_out
    )
    top_grad = lax.psum(top_part, ("grp", "row"))
    owned = lax.psum_scatter(hot_part, "row", scatter_dimension=0, tiled=True).reshape(
        count, BLOCK, width
    )
    quarter = lax.axis_index("grp")
    groups = lax.axis_size("grp")
    per_owner = total_blocks // groups
    arrived, arrived_ids = (
        lax.all_gather(owned, "grp", axis=0, tiled=True),
        lax.all_gather(chosen.astype(jnp.float32), "grp", axis=0, tiled=True),
    )
    slot = arrived_ids.astype(jnp.int32) - quarter * per_owner
    inside = (slot >= 0) & (slot < per_owner)
    slot = jnp.where(inside, slot, per_owner)
    grad = (
        jnp.zeros((per_owner, BLOCK, width), jnp.float32)
        .at[slot]
        .add(arrived, mode="drop")
        .reshape(-1, width)
    )
    weights = master[0]
    state = accum[0]
    new_state = state + jnp.mean(grad * grad, axis=1)
    new_weights = weights - lr_step * grad / jnp.sqrt(new_state)[:, None]
    scale_new = (
        jnp.max(jnp.abs(new_weights.reshape(per_owner, BLOCK * width)), axis=1) + 1e-06
    ).astype(jnp.bfloat16)
    coded = (
        (
            new_weights.reshape(per_owner, BLOCK, width)
            / scale_new.astype(jnp.float32)[:, None, None]
        )
        .astype(jnp.bfloat16)
        .reshape(-1, width)
    )
    fresh, fresh_scale = (
        lax.all_gather(coded, "grp", axis=0, tiled=True),
        lax.all_gather(scale_new, "grp", axis=0, tiled=True),
    )
    return (new_weights[None], new_state[None], fresh, fresh_scale, top_grad)


def solution(mesh):
    return jax.shard_map(
        on_device,
        mesh=mesh,
        in_specs=(
            P("row", None),
            P("row"),
            P("grp", "row"),
            P(("grp", "row"), None),
            P(("grp", "row"), None),
            P(("grp", "row"), None),
            P(("grp", "row")),
            P(),
            P(),
            P("grp", "row", None),
            P("grp", "row"),
        ),
        out_specs=(P("grp", "row", None), P("grp", "row"), P("row", None), P("row"), P()),
        check_vma=False,
    )
```

profile of v0, /device:TPU:0, one launch (start us, length us, event | category | flops | bytes accessed | tf_op | source)
XLA Modules:
  0.0 261.1 jit_solution(4268729098067179809)
XLA Ops:
  8.0 0.0 reduce-scatter.2.cloned.1.call-start
  8.1 1.0 reduce-window.9
  9.1 0.1 slice.10
  9.2 0.1 slice_reduce_fusion
  9.3 0.8 bitcast_subtract_fusion
  10.1 0.1 compare_select_fusion
  10.2 0.1 reshape.249
  10.4 16.7 %gather_fusion = s32[4096]{0:T(1024)S(1)} fusion(s32[1024]{0:T(1024)S(1)} %bitcast.46, s32[4096]{0:T(1024)S(1)} %broadcast_clamp_fusion), kind=kCustom, calls=%fused_computation | custom fusion | bytes 49152 | tf_op jit(solution)/shard_map/gather | solution.py:19
  27.1 0.1 reshape.248
  27.2 0.1 fusion.8
  27.3 0.6 dynamic-slice.2
  28.6 0.6 gather_fusion.2
  29.2 0.2 dynamic-update-slice.1
  29.5 10.4 %fusion.1 = bf16[256,2048]{1,0:T(8,128)(2,1)S(1)} fusion(s32[256,16]{1,0:T(8,128)S(1)} %fusion.8), kind=kLoop, calls=%fused_computation.6 | loop fusion | flops 24641536 | bytes 1064960 | tf_op jit(solution)/shard_map/while/body/eval_jaxpr/reduce_sum | solution.py:25
  39.9 18.1 %all-reduce.1 = bf16[16]{0:T(256)(128)(2,1)S(1)} all-reduce(bf16[16]{0:T(256)(128)(2,1)S(1)} %dynamic-update-slice.1), channel_id=4, replica_groups=mesh['grp'=4,'row'=8] {'row'}, use_global_device_ids=true, to_apply=%add.1 | all-reduce | flops 16 | bytes 64
  58.0 0.6 gather_fusion.1
  58.6 15.1 %all-gather.1 = bf16[16,128,128]{2,1,0:T(8,128)(2,1)S(1)} all-gather(bf16[2,128,128]{2,1,0:T(8,128)(2,1)S(1)} %gather_fusion.1), channel_id=3, replica_groups=mesh['grp'=4,'row'=8] {'row'}, dimensions={0}, use_global_device_ids=true | all-gather | bytes 589824 | tf_op jit(solution)/shard_map/all_gather | solution.py:89
  73.7 0.1 copy.19
  73.8 0.1 convert_multiply_fusion
  74.0 1.0 convolution_convert_fusion
  75.0 0.0 copy-done.3
  75.0 0.3 fusion.10
  75.3 0.4 copy-done.9
  75.7 1.1 fusion.2
  76.8 0.4 multiply_convert_fusion
  77.2 0.3 fusion.5
  77.5 2.2 fusion.18
  79.7 0.0 all-reduce.5.cloned.1.call-start
  79.8 0.6 copy-done.12
  80.3 0.6 dynamic-slice.1
  81.6 0.1 bitcast_dynamic-update-slice_fusion
  81.7 9.9 %all-reduce = f32[8]{0:T(128)S(1)} all-reduce(f32[8]{0:T(128)S(1)} %bitcast_dynamic-update-slice_fusion), channel_id=2, replica_groups=mesh['grp'=4,'row'=8] {'grp'}, use_global_device_ids=true, to_apply=%add | all-reduce | flops 8 | bytes 64
  92.2 1.3 fusion.9
  93.5 17.2 %reduce-scatter.2.cloned.1.call-done = f32[256,128]{1,0:T(8,128)} async-done(((f32[2048,128]{1,0:T(8,128)}), f32[256,128]{1,0:T(8,128)}) %reduce-scatter.2.cloned.1.call-update) | async-done | bytes 131088 | tf_op jit(solution)/shard_map/reduce_scatter | solution.py:99
  110.8 10.3 %all_gather.21 = f32[8,128,128]{2,1,0:T(8,128)S(1)} all-gather(f32[2,128,128]{2,1,0:T(8,128)} %bitcast.51), channel_id=1, replica_groups=mesh['grp'=4,'row'=8] {'grp'}, dimensions={0}, use_global_device_ids=true | all-gather | bytes 655360 | tf_op jit(solution)/shard_map/all_gather | solution.py:106
  121.1 1.0 scatter_fusion
  122.2 0.1 broadcast_multiply_fusion
  122.4 0.8 abs_reduce_fusion
  123.2 0.1 bitcast_reduce_fusion
  123.3 0.2 dynamic-update-slice.2
  123.6 9.6 %all-reduce.2 = bf16[16]{0:T(256)(128)(2,1)} all-reduce(bf16[16]{0:T(256)(128)(2,1)S(1)} %dynamic-update-slice.2), channel_id=1, replica_groups=mesh['grp'=4,'row'=8] {'grp'}, use_global_device_ids=true, to_apply=%add.2 | all-reduce | flops 16 | bytes 64
  133.3 0.2 divide_convert_fusion
  133.4 9.7 %all_gather.22 = bf16[2048,128]{1,0:T(8,128)(2,1)S(1)} all-gather(bf16[512,128]{1,0:T(8,128)(2,1)S(1)} %bitcast.50), channel_id=1, replica_groups=mesh['grp'=4,'row'=8] {'grp'}, dimensions={0}, use_global_device_ids=true | all-gather | bytes 655360 | tf_op jit(solution)/shard_map/all_gather | solution.py:134
  143.1 0.6 add.103
  143.6 107.6 %all-reduce.5.cloned.1.call-done = f32[256,1024]{1,0:T(8,128)} async-done(((f32[256,1024]{1,0:T(8,128)}), f32[256,1024]{1,0:T(8,128)}) %all-reduce.5.cloned.1.call-update) | async-done | bytes 1048592 | tf_op jit(solution)/shard_map/psum | solution.py:98
  251.3 0.8 copy.26
  252.1 0.6 copy-done.5
  252.7 1.0 copy.27
  (40 shorter events, 0.2 us)
Async XLA Ops:
  8.0 50.0 %copy-start = (bf16[2048,128]{1,0:T(8,128)(2,1)S(1)}, bf16[2048,128]{1,0:T(8,128)(2,1)}, u32[]{:S(2)}) copy-start(bf16[2048,128]{1,0:T(8,128)(2,1)} %param.11) | copy-start | bytes 1572868
  8.0 2.3 copy-start.1
  8.0 102.7 %reduce-scatter.2.cloned.1.call-start = ((), (), s32[]{:S(2)}) async-start(), calls=%async_computation.1 | async-start | bytes 1179648 | tf_op jit(solution)/shard_map/reduce_scatter | solution.py:99
  10.3 16.8 %copy-start.8 = (s32[1,256]{1,0:T(1,128)S(1)}, s32[1,256]{1,0:T(1,128)}, u32[]{:S(2)}) copy-start(s32[1,256]{1,0:T(1,128)} %param.14) | copy-start | bytes 3076
  10.3 16.9 %copy-start.11 = (s32[1,2]{1,0:T(1,128)S(1)}, s32[1,2]{1,0:T(1,128)}, u32[]{:S(2)}) copy-start(s32[1,2]{1,0:T(1,128)} %param.13) | copy-start | bytes 28
  10.3 17.0 %copy-start.13 = (u32[32]{0:T(128)S(1)}, u32[32]{0:T(128)}, u32[]{:S(2)}) copy-start(u32[32]{0:T(128)} %constant.82) | copy-start | bytes 388
  10.4 18.2 %copy-start.2 = (bf16[16]{0:T(256)(128)(2,1)S(1)}, bf16[16]{0:T(256)(128)(2,1)}, u32[]{:S(2)}) copy-start(bf16[16]{0:T(256)(128)(2,1)} %param.12) | copy-start | bytes 100
  29.2 44.5 %copy-start.6 = (bf16[256,128]{1,0:T(8,128)(2,1)S(1)}, bf16[256,128]{1,0:T(8,128)(2,1)}, u32[]{:S(2)}) copy-start(bf16[256,128]{1,0:T(8,128)(2,1)} %param.16) | copy-start | bytes 196612
  73.9 1.0 copy-start.3
  75.0 0.7 copy-start.9
  75.7 1.1 copy-start.10
  79.7 0.7 copy-start.12
  79.7 171.5 %all-reduce.5.cloned.1.call-start = ((), (), s32[]{:S(2)}) async-start(), calls=%async_computation.2 | async-start | bytes 2097152 | tf_op jit(solution)/shard_map/psum | solution.py:98
  121.1 1.2 copy-start.7
  121.1 1.2 copy-start.4
  251.3 1.4 copy-start.5
Sparse Core Ops, SparseCore 0:
  79.8 30.8 reduce-scatter.1
Sparse Core Ops, SparseCore 1:
  123.7 127.5 all-reduce.4
where the time goes:
time: 262 us; the launch traced here: 261 us
  waiting for transfers between devices  125 us (48%)
  blocking collectives  72.7 us (28%)
  local copies, waits for them, and re-layouts  23.5 us (9%)
  between operations  17.8 us (7%)
  other arithmetic  16 us (6%)
  matrix products  6.17 us (2%)
    psum x1, waiting for transfers between devices, on_device(): top_grad = lax.psum(top_part, ('grp', 'row'))  108 us
    unnamed x3, blocking collectives  37.6 us
    reduce_scatter x1, waiting for transfers between devices, on_device(): lax.psum_scatter(hot_part, 'row', scatter_dimension=0, tiled=True)  17.2 us
    gather x2, local copies, waits for them, and re-layouts, pool_grad(): indices[positions]  16.8 us
    all_gather x1, blocking collectives, on_device(): lax.all_gather(picked, 'row', axis=0, tiled=True)  15.1 us
    reduce_sum x1, other arithmetic, count_block(): jnp.sum((picked[:, :, None] == columns[None, None, :]).astype(jnp.bfloat1...  10.4 us
    all_gather x1, blocking collectives, on_device(): lax.all_gather(owned, 'grp', axis=0, tiled=True)  10.3 us
    all_gather x1, blocking collectives, on_device(): lax.all_gather(coded, 'grp', axis=0, tiled=True)  9.65 us
  transfers between devices with their start and end apart: 2, of which 2 were waited for; matrix products, arithmetic and copies ran while one was open for 1% of the time, Pallas kernels for 0%

commit v1 on v0

--- a/solution.py
+++ b/solution.py
@@ -95,7 +95,7 @@
     top_part, hot_part, used_rows = pool_grad(
         table, bag_lengths[0], bag_indices[0], dense_act, labels, w_top, w_out
     )
-    top_grad = lax.psum(top_part, ("grp", "row"))
+    top_grad = lax.psum(lax.psum(top_part, "row"), "grp")
     owned = lax.psum_scatter(hot_part, "row", scatter_dimension=0, tiled=True).reshape(
         count, BLOCK, width
     )

time: 262 us -> 235 us (0.90)
  waiting for transfers between devices: 125 us -> 97.6 us
  blocking collectives: 72.7 us -> 75.5 us
    psum x1 -> x2, waiting for transfers between devices: 108 us -> 63 us  [on_device(): top_grad = lax.psum(lax.psum(top_part, 'row'), 'grp')]
    reduce_scatter x1, waiting for transfers between devices: 17.2 us -> 34.6 us  [on_device(): lax.psum_scatter(hot_part, 'row', scatter_dimension=0, tiled=True)]
    all_gather x1, blocking collectives: 10.3 us -> 13.1 us  [on_device(): lax.all_gather(owned, 'grp', axis=0, tiled=True)]
  transfers between devices with their start and end apart: 2 -> 3, of which waited for: 2 -> 3; matrix products, arithmetic and copies ran while one was open for 1% -> 3% of each run, Pallas kernels for 0% -> 0%
where the time goes in v1:
time: 235 us
  waiting for transfers between devices  97.6 us (42%)
  blocking collectives  75.5 us (32%)
  local copies, waits for them, and re-layouts  23.5 us (10%)
  other arithmetic  16 us (7%)
  between operations  16 us (7%)
  matrix products  6.21 us (3%)
    psum x2, waiting for transfers between devices, on_device(): top_grad = lax.psum(lax.psum(top_part, 'row'), 'grp')  63 us
    unnamed x3, blocking collectives  37.5 us
    reduce_scatter x1, waiting for transfers between devices, on_device(): lax.psum_scatter(hot_part, 'row', scatter_dimension=0, tiled=True)  34.6 us
    gather x2, local copies, waits for them, and re-layouts, pool_grad(): indices[positions]  16.8 us
    all_gather x1, blocking collectives, on_device(): lax.all_gather(picked, 'row', axis=0, tiled=True)  15.1 us
    all_gather x1, blocking collectives, on_device(): lax.all_gather(owned, 'grp', axis=0, tiled=True)  13.1 us
    reduce_sum x1, other arithmetic, count_block(): jnp.sum((picked[:, :, None] == columns[None, None, :]).astype(jnp.bfloat1...  10.4 us
    all_gather x1, blocking collectives, on_device(): lax.all_gather(coded, 'grp', axis=0, tiled=True)  9.74 us
  transfers between devices with their start and end apart: 3, of which 3 were waited for; matrix products, arithmetic and copies ran while one was open for 3% of the time, Pallas kernels for 0%

profile of v1, /device:TPU:0, one launch (start us, length us, event | category | flops | bytes accessed | tf_op | source)
XLA Modules:
  0.0 234.9 jit_solution(3792107413024497601)
XLA Ops:
  7.2 1.0 reduce-window.9
  8.3 0.1 slice.10
  8.4 0.1 slice_reduce_fusion
  8.5 0.8 bitcast_subtract_fusion
  9.3 0.1 compare_select_fusion
  9.4 0.1 reshape.249
  9.5 16.7 %gather_fusion = s32[4096]{0:T(1024)S(1)} fusion(s32[1024]{0:T(1024)S(1)} %bitcast.46, s32[4096]{0:T(1024)S(1)} %broadcast_clamp_fusion), kind=kCustom, calls=%fused_computation | custom fusion | bytes 49152 | tf_op jit(solution)/shard_map/gather | solution.py:19
  26.2 0.1 reshape.248
  26.3 0.1 fusion.8
  26.5 0.6 dynamic-slice.2
  27.7 0.6 gather_fusion.2
  28.4 0.2 dynamic-update-slice.1
  28.6 10.4 %fusion.1 = bf16[256,2048]{1,0:T(8,128)(2,1)S(1)} fusion(s32[256,16]{1,0:T(8,128)S(1)} %fusion.8), kind=kLoop, calls=%fused_computation.6 | loop fusion | flops 24641536 | bytes 1064960 | tf_op jit(solution)/shard_map/while/body/eval_jaxpr/reduce_sum | solution.py:25
  39.0 18.1 %all-reduce.1 = bf16[16]{0:T(256)(128)(2,1)S(1)} all-reduce(bf16[16]{0:T(256)(128)(2,1)S(1)} %dynamic-update-slice.1), channel_id=4, replica_groups=mesh['grp'=4,'row'=8] {'row'}, use_global_device_ids=true, to_apply=%add.1 | all-reduce | flops 16 | bytes 64
  57.2 0.6 gather_fusion.1
  57.7 15.1 %all-gather.1 = bf16[16,128,128]{2,1,0:T(8,128)(2,1)S(1)} all-gather(bf16[2,128,128]{2,1,0:T(8,128)(2,1)S(1)} %gather_fusion.1), channel_id=3, replica_groups=mesh['grp'=4,'row'=8] {'row'}, dimensions={0}, use_global_device_ids=true | all-gather | bytes 589824 | tf_op jit(solution)/shard_map/all_gather | solution.py:89
  72.9 0.1 copy.19
  73.0 0.1 convert_multiply_fusion
  73.1 1.0 convolution_convert_fusion
  74.2 0.3 fusion.10
  74.5 0.4 copy-done.9
  74.8 1.1 fusion.2
  76.0 0.4 multiply_convert_fusion
  76.4 1.3 fusion.9
  77.7 0.0 reduce-scatter.2.cloned.1.call-start
  77.8 0.3 fusion.5
  78.1 2.2 fusion.18
  80.3 0.0 all-reduce.8.cloned.1.call-start
  80.3 0.6 copy-done.12
  80.9 0.6 dynamic-slice.1
  82.2 0.1 bitcast_dynamic-update-slice_fusion
  82.3 9.9 %all-reduce = f32[8]{0:T(128)S(1)} all-reduce(f32[8]{0:T(128)S(1)} %bitcast_dynamic-update-slice_fusion), channel_id=2, replica_groups=mesh['grp'=4,'row'=8] {'grp'}, use_global_device_ids=true, to_apply=%add | all-reduce | flops 8 | bytes 64
  92.8 42.7 %all-reduce.6.cloned.1.call-done = f32[256,1024]{1,0:T(8,128)} async-done(((f32[256,1024]{1,0:T(8,128)}), f32[256,1024]{1,0:T(8,128)}) %all-reduce.6.cloned.1.call-update) | async-done | bytes 1048592 | tf_op jit(solution)/shard_map/psum | solution.py:98
  135.5 34.6 %reduce-scatter.2.cloned.1.call-done = f32[256,128]{1,0:T(8,128)} async-done(((f32[2048,128]{1,0:T(8,128)}), f32[256,128]{1,0:T(8,128)}) %reduce-scatter.2.cloned.1.call-update) | async-done | bytes 131088 | tf_op jit(solution)/shard_map/reduce_scatter | solution.py:99
  170.1 13.1 %all_gather.21 = f32[8,128,128]{2,1,0:T(8,128)S(1)} all-gather(f32[2,128,128]{2,1,0:T(8,128)} %bitcast.51), channel_id=1, replica_groups=mesh['grp'=4,'row'=8] {'grp'}, dimensions={0}, use_global_device_ids=true | all-gather | bytes 655360 | tf_op jit(solution)/shard_map/all_gather | solution.py:106
  183.2 1.0 scatter_fusion
  184.3 0.1 broadcast_multiply_fusion
  184.5 0.8 abs_reduce_fusion
  185.3 0.1 bitcast_reduce_fusion
  185.4 0.2 dynamic-update-slice.2
  185.7 9.5 %all-reduce.2 = bf16[16]{0:T(256)(128)(2,1)} all-reduce(bf16[16]{0:T(256)(128)(2,1)S(1)} %dynamic-update-slice.2), channel_id=1, replica_groups=mesh['grp'=4,'row'=8] {'grp'}, use_global_device_ids=true, to_apply=%add.2 | all-reduce | flops 16 | bytes 64
  195.2 0.2 divide_convert_fusion
  195.4 9.7 %all_gather.22 = bf16[2048,128]{1,0:T(8,128)(2,1)S(1)} all-gather(bf16[512,128]{1,0:T(8,128)(2,1)S(1)} %bitcast.50), channel_id=1, replica_groups=mesh['grp'=4,'row'=8] {'grp'}, dimensions={0}, use_global_device_ids=true | all-gather | bytes 655360 | tf_op jit(solution)/shard_map/all_gather | solution.py:134
  205.1 0.6 add.105
  205.7 20.3 %all-reduce.8.cloned.1.call-done = f32[256,1024]{1,0:T(8,128)} async-done(((f32[256,1024]{1,0:T(8,128)}), f32[256,1024]{1,0:T(8,128)}) %all-reduce.8.cloned.1.call-update) | async-done | bytes 1048592 | tf_op jit(solution)/shard_map/psum | solution.py:98
  225.9 0.8 copy.27
  226.7 0.6 copy-done.5
  227.4 1.0 copy.28
  (43 shorter events, 0.3 us)
Async XLA Ops:
  7.2 50.0 %copy-start = (bf16[2048,128]{1,0:T(8,128)(2,1)S(1)}, bf16[2048,128]{1,0:T(8,128)(2,1)}, u32[]{:S(2)}) copy-start(bf16[2048,128]{1,0:T(8,128)(2,1)} %param.11) | copy-start | bytes 1572868
  7.2 2.3 copy-start.1
  7.2 128.3 %all-reduce.6.cloned.1.call-start = ((), (), s32[]{:S(2)}) async-start(), calls=%async_computation.2 | async-start | bytes 2097152 | tf_op jit(solution)/shard_map/psum | solution.py:98
  9.5 16.8 %copy-start.8 = (s32[1,256]{1,0:T(1,128)S(1)}, s32[1,256]{1,0:T(1,128)}, u32[]{:S(2)}) copy-start(s32[1,256]{1,0:T(1,128)} %param.14) | copy-start | bytes 3076
  9.5 16.9 %copy-start.11 = (s32[1,2]{1,0:T(1,128)S(1)}, s32[1,2]{1,0:T(1,128)}, u32[]{:S(2)}) copy-start(s32[1,2]{1,0:T(1,128)} %param.13) | copy-start | bytes 28
  9.5 17.0 %copy-start.13 = (u32[32]{0:T(128)S(1)}, u32[32]{0:T(128)}, u32[]{:S(2)}) copy-start(u32[32]{0:T(128)} %constant.82) | copy-start | bytes 388
  9.5 18.2 %copy-start.2 = (bf16[16]{0:T(256)(128)(2,1)S(1)}, bf16[16]{0:T(256)(128)(2,1)}, u32[]{:S(2)}) copy-start(bf16[16]{0:T(256)(128)(2,1)} %param.12) | copy-start | bytes 100
  28.4 44.5 %copy-start.6 = (bf16[256,128]{1,0:T(8,128)(2,1)S(1)}, bf16[256,128]{1,0:T(8,128)(2,1)}, u32[]{:S(2)}) copy-start(bf16[256,128]{1,0:T(8,128)(2,1)} %param.16) | copy-start | bytes 196612
  73.1 1.0 copy-start.3
  74.2 0.7 copy-start.9
  74.8 1.1 copy-start.10
  77.7 92.4 %reduce-scatter.2.cloned.1.call-start = ((), (), s32[]{:S(2)}) async-start(), calls=%async_computation.1 | async-start | bytes 1179648 | tf_op jit(solution)/shard_map/reduce_scatter | solution.py:99
  80.3 0.7 copy-start.12
  80.3 145.7 %all-reduce.8.cloned.1.call-start = ((), (), s32[]{:S(2)}) async-start(), calls=%async_computation.3 | async-start | bytes 2097152 | tf_op jit(solution)/shard_map/psum | solution.py:98
  183.2 1.2 copy-start.7
  183.2 1.2 copy-start.4
  225.9 1.4 copy-start.5
Sparse Core Ops, SparseCore 0:
  77.9 57.6 all-reduce.5
  138.4 31.6 reduce-scatter.1
  173.2 52.7 all-reduce.7
